TPU v7x, 256 devices: a whole 4x4x8 slice. The times are simulated.
256 devices in a mesh: ctx: 16 (over z_hi, x, core), exp: 16 (over y, z_lo).
Axes of the slice: x: 4, y: 4, z: 8 (z_hi: 2, z_lo: 4; z = z_hi * 4 + z_lo), core: 2. Of those that a mesh axis runs over, the one named last changes fastest.
Arguments:
- q_nope: bfloat16 [1024, 128, 512], P('ctx', 'exp'), may hold values from -72 to 72
- q_rope: bfloat16 [1024, 8192], P('ctx', 'exp'), may hold values from -6 to 6
- cache_keys: bfloat16 [576, 2048], P(None, 'ctx'), may hold values from -6 to 6
- fresh_keys: bfloat16 [576, 1024], P(None, 'ctx'), may hold values from -6 to 6
- block_order: int32 [32], replicated, may hold values from 0 to 31, each once
- w_uv: bfloat16 [128, 512, 128], P('exp'), may hold values from -0.25 to 0.25
- w_out: bfloat16 [16384, 7168], P('exp', 'ctx'), may hold values from -0.046875 to 0.046875
- residual: bfloat16 [1024, 7168], P(('ctx', 'exp')), may hold values from -6 to 6
- norm_gain: float32 [7168], replicated, may hold values from 0.5 to 1.5
- router_weight: bfloat16 [7168, 16], replicated, may hold values from -0.0625 to 0.0625
- expert_ids: int32 [1024, 8], P(('ctx', 'exp')), may hold values from 0 to 15, all different within a row; in each aligned block of 4 rows (0 to 3, 4 to 7, ...) at most 3 rows name the same one
- w_gate: bfloat16 [16, 7168, 2048], P('exp', None, 'ctx'), may hold values from -0.0625 to 0.0625
- w_up: bfloat16 [16, 7168, 2048], P('exp', None, 'ctx'), may hold values from -0.0625 to 0.0625
- w_down: bfloat16 [16, 2048, 7168], P('exp', 'ctx'), may hold values from -0.125 to 0.125
Outputs:
- layer_out: bfloat16 [1024, 7168], P(('ctx', 'exp'))
Inputs may be any that keep to these rules, and one draw needn't show every extreme that they name: A permutation: block j of the new tokens (32 rows) sits at positions 2048 + block_order[j] * 32 onward. `expert_ids`: each row names 8 different experts; the 4 rows of one device name no expert more than 3 times, and in some aligned block one expert exactly 3 times.
All inputs are finite; a program needn't handle non-finite values.
Results may differ from a plain program's by a relative error of at most 0.012.
Values may be sent and summed in bfloat16 or wider, within the bound.
A program may use at most 128 MiB of HBM per device.

v0:
```python
import math
import jax
import jax.numpy as jnp
from jax import lax
from jax.sharding import PartitionSpec as P

QKD = 192
CAP = 3
ROUTE_SCALE = 2.5
NORM_EPS = 1e-06


def copy_for_each(value, axis):
    copies = jnp.broadcast_to(value, (lax.axis_size(axis), *value.shape))
    return lax.all_to_all(copies, axis, split_axis=0, concat_axis=0, tiled=True)


def in_order(pieces, dim):
    pieces = jnp.moveaxis(pieces, 0, dim)
    shape = pieces.shape
    return pieces.reshape(*shape[:dim], shape[dim] * shape[dim + 1], *shape[dim + 2 :])


def gather_directly(value, axis, dim):
    pieces = copy_for_each(value, axis)
    return in_order(pieces, dim)


def in_blocks(value, dim, length):
    shape = value.shape
    pieces = value.reshape(*shape[:dim], length, shape[dim] // length, *shape[dim + 1 :])
    return jnp.moveaxis(pieces, dim, 0)


def sum_at_owner(value, axis, dim):
    length = lax.axis_size(axis)
    pieces = lax.all_to_all(in_blocks(value, dim, length), axis, 0, 0, tiled=True)
    return jnp.sum(pieces.astype(jnp.float32), axis=0)


def block_position(row_index, block_order, block_rows):
    blocks = row_index // block_rows
    lookup = blocks[:, None] == jnp.arange(block_order.shape[0], dtype=jnp.int32)[None, :]
    leading = jnp.sum(jnp.where(lookup, block_order[None, :], 0), axis=1)
    return leading * block_rows + row_index % block_rows


def attend(query_lat, query_pe, keys, visible):
    row_count, head_count, latent_width = query_lat.shape
    key_count = keys.shape[1]
    pe_width = query_pe.shape[1] // head_count
    first_dot = jnp.dot(
        query_lat.reshape(row_count * head_count, latent_width),
        keys[:latent_width],
        preferred_element_type=jnp.float32,
    )
    second_dot = jnp.dot(
        query_pe.reshape(row_count * head_count, pe_width),
        keys[latent_width:],
        preferred_element_type=jnp.float32,
    )
    scores = ((first_dot + second_dot) * (1.0 / math.sqrt(QKD))).reshape(
        row_count, head_count, key_count
    )
    scores = jnp.where(visible[:, None, :], scores, -jnp.inf)
    row_max = jnp.max(scores, axis=2)
    exponent = jnp.exp(scores - row_max[:, :, None])
    row_sum = jnp.sum(exponent, axis=2)
    weights = exponent.astype(jnp.bfloat16).reshape(row_count * head_count, key_count)
    latent = lax.dot_general(
        weights, keys[:latent_width], (((1,), (1,)), ((), ())), preferred_element_type=jnp.float32
    )
    return (row_max, row_sum, latent.reshape(row_count, head_count, latent_width))


def merge_partial(earlier, latter):
    highest = latter[0]
    earlier_scale = jnp.exp(earlier[0] - highest)
    latter_scale = jnp.exp(latter[0] - highest)
    row_sum = earlier_scale * earlier[1] + latter_scale * latter[1]
    latent = earlier_scale[:, :, None] * earlier[2] + latter_scale[:, :, None] * latter[2]
    return (highest, row_sum, latent)


def body(
    q_nope,
    q_rope,
    cache_keys,
    fresh_keys,
    block_order,
    w_uv,
    w_out,
    residual,
    norm_gain,
    router_weight,
    expert_ids,
    w_gate,
    w_up,
    w_down,
):
    ctx_count = lax.axis_size("ctx")
    exp_count = lax.axis_size("exp")
    ctx_index = lax.axis_index("ctx")
    rows_here, heads_here, latent_width = q_nope.shape
    value_width = w_uv.shape[2]
    cache_len = cache_keys.shape[1]
    key_cols = cache_len + rows_here
    block_rows = rows_here // 2
    keys_here = jnp.concatenate([cache_keys, fresh_keys], axis=1)
    w_uv_wide = w_uv.astype(jnp.float32)
    own_rows = ctx_index * rows_here + jnp.arange(rows_here, dtype=jnp.int32)
    own_pos = block_position(own_rows, block_order, block_rows)
    start_state = (
        jnp.full((rows_here, heads_here), -jnp.inf, jnp.float32),
        jnp.zeros((rows_here, heads_here), jnp.float32),
        jnp.zeros((rows_here, heads_here, latent_width), jnp.float32),
    )
    portion = lax.all_gather(keys_here, "ctx", axis=1, tiled=True)
    columns = jnp.arange(portion.shape[1], dtype=jnp.int32)
    owner_dev = columns // key_cols
    within = columns % key_cols
    fresh_row = owner_dev * rows_here + within - cache_len
    key_pos = jnp.where(within < cache_len, -1, block_position(fresh_row, block_order, block_rows))
    visible = key_pos[None, :] <= own_pos[:, None]
    row_max, row_sum, latent = merge_partial(start_state, attend(q_nope, q_rope, portion, visible))
    normal_lat = latent / row_sum[:, :, None]
    head_wide = jnp.einsum("rhl,hlv->rhv", normal_lat, w_uv_wide, precision=lax.Precision.HIGHEST)
    head_out = head_wide.astype(jnp.bfloat16).reshape(rows_here, heads_here * value_width)
    tok_here, model_width = residual.shape
    col_part = w_out.shape[1]
    head_partial = jnp.dot(
        gather_directly(head_out, "ctx", 0), w_out, preferred_element_type=jnp.float32
    )
    arranged = head_partial.reshape(ctx_count, exp_count, tok_here, col_part)
    head_total = sum_at_owner(arranged.astype(jnp.bfloat16), "exp", 1)
    attention = lax.all_to_all(
        head_total.astype(jnp.bfloat16), "ctx", split_axis=0, concat_axis=3, tiled=True
    ).reshape(tok_here, model_width)
    hidden = residual.astype(jnp.float32) + attention.astype(jnp.float32)
    mean_square = jnp.mean(hidden * hidden, axis=1, keepdims=True)
    normed = (hidden * lax.rsqrt(mean_square + NORM_EPS) * norm_gain).astype(jnp.bfloat16)
    affinity = jax.nn.sigmoid(jnp.dot(normed, router_weight, preferred_element_type=jnp.float32))
    expert_count = router_weight.shape[1]
    onehot = expert_ids[:, :, None] == jnp.arange(expert_count, dtype=jnp.int32)[None, None, :]
    chosen = jnp.sum(jnp.where(onehot, affinity[:, None, :], 0.0), axis=2)
    route = ROUTE_SCALE * chosen / jnp.sum(chosen, axis=1, keepdims=True)
    mixing = jnp.sum(jnp.where(onehot, route[:, :, None], 0.0), axis=1)
    picked = jnp.sum(onehot.astype(jnp.int32), axis=1)
    slot_index = jnp.cumsum(picked, axis=0) - picked
    slot_hot = (slot_index[:, :, None] == jnp.arange(CAP, dtype=jnp.int32)[None, None, :]) & (
        picked[:, :, None] > 0
    )
    dispatch_map = (
        jnp.transpose(slot_hot, (1, 2, 0))
        .reshape(expert_count * CAP, tok_here)
        .astype(jnp.bfloat16)
    )
    send_rows = jnp.dot(dispatch_map, normed, preferred_element_type=jnp.float32).astype(
        jnp.bfloat16
    )
    arrived = lax.all_to_all(
        send_rows.reshape(expert_count, CAP, model_width),
        "exp",
        split_axis=0,
        concat_axis=1,
        tiled=True,
    )
    local_experts = arrived.shape[0]
    portion = lax.all_gather(arrived, "ctx", axis=1, tiled=True)
    gate = jnp.einsum("end,edf->enf", portion, w_gate, preferred_element_type=jnp.float32)
    upward = jnp.einsum("end,edf->enf", portion, w_up, preferred_element_type=jnp.float32)
    activations = (jax.nn.silu(gate) * upward).astype(jnp.bfloat16)
    expert_total = lax.psum_scatter(
        jnp.einsum("enf,efd->ned", activations, w_down, preferred_element_type=jnp.float32).astype(
            jnp.bfloat16
        ),
        "ctx",
        scatter_dimension=0,
        tiled=True,
    )
    going_back = expert_total.reshape(exp_count, CAP, local_experts, model_width)
    returned = lax.all_to_all(going_back, "exp", split_axis=0, concat_axis=2, tiled=True)
    combine_map = jnp.where(slot_hot, mixing[:, :, None], 0.0)
    combine_map = jnp.transpose(combine_map, (0, 2, 1)).reshape(tok_here, CAP * expert_count)
    mixture = jnp.dot(
        combine_map,
        returned.reshape(CAP * expert_count, model_width).astype(jnp.float32),
        precision=lax.Precision.HIGHEST,
    )
    return (hidden + mixture).astype(jnp.bfloat16)


def solution(mesh):
    return jax.shard_map(
        body,
        mesh=mesh,
        in_specs=(
            P("ctx", "exp", None),
            P("ctx", "exp"),
            P(None, "ctx"),
            P(None, "ctx"),
            P(),
            P("exp", None, None),
            P("exp", "ctx"),
            P(("ctx", "exp"), None),
            P(),
            P(),
            P(("ctx", "exp"), None),
            P("exp", None, "ctx"),
            P("exp", None, "ctx"),
            P("exp", "ctx", None),
        ),
        out_specs=P(("ctx", "exp"), None),
        check_vma=False,
    )
```

profile of v0, /device:TPU:1, one launch (start us, length us, event | category | flops | bytes accessed | tf_op | source)
XLA Modules:
  0.0 590.2 jit_solution(14569055627388049429)
XLA Ops:
  6.5 1.2 copy.37
  7.7 1.6 pad_maximum_fusion
  12.2 77.7 %all-gather.3.cloned.1.call-done = bf16[576,3072]{0,1:T(8,128)(2,1)} async-done(((bf16[576,192]{0,1:T(8,128)(2,1)}), bf16[576,3072]{0,1:T(8,128)(2,1)}) %all-gather.3.cloned.1.call-update) | async-done | bytes 3538960 | tf_op jit(solution)/shard_map/all_gather | solution.py:118
  89.8 3.9 fusion.13
  93.7 3.1 fusion.90
  96.8 2.6 copy-done.1
  100.8 5.6 fusion.37
  106.4 1.2 fusion.56
  108.0 37.4 %all_to_all.46 = bf16[16,64,1024]{2,1,0:T(8,128)(2,1)S(1)} all-to-all(bf16[16,64,1024]{2,1,0:T(8,128)(2,1)S(1)} %broadcast_in_dim.120), channel_id=1, replica_groups=mesh['ctx'=16,'exp'=16] {'ctx'}, dimensions={0} | all-to-all | bytes 4194304 | tf_op jit(solution)/shard_map/all_to_all | solution.py:15
  146.5 1.4 fusion.24
  148.0 1.8 copy.43
  149.8 24.8 %all-to-all-start.1 = ((bf16[16,16,1,4,448]{4,3,1,2,0:T(4,128)(2,1)}), bf16[16,16,1,4,448]{4,3,1,2,0:T(4,128)(2,1)S(1)}, u32[]{:S(2)}, u32[]{:S(2)}) async-start(bf16[16,16,1,4,448]{4,3,1,2,0:T(4,128)(2,1)} %copy.43), calls=%async_computation.1 | async-start | bytes 2097152 | tf_op jit(solution)/shard_map/all_to_all | solution.py:37
  174.7 27.0 %all-to-all-done.1 = bf16[16,16,1,4,448]{4,3,1,2,0:T(4,128)(2,1)S(1)} async-done(((bf16[16,16,1,4,448]{4,3,1,2,0:T(4,128)(2,1)}), bf16[16,16,1,4,448]{4,3,1,2,0:T(4,128)(2,1)S(1)}, u32[]{:S(2)}, u32[]{:S(2)}) %all-to-all-start.1) | async-done | bytes 917536 | tf_op jit(solution)/shard_map/all_to_all | solution.py:37
  202.8 5.3 all-to-all-start.2
  208.6 9.2 %all-to-all-done.2 = bf16[16,1,4,448]{3,2,1,0:T(4,128)(2,1)S(1)} async-done(((bf16[16,1,4,448]{3,2,1,0:T(4,128)(2,1)}), bf16[16,1,4,448]{3,2,1,0:T(4,128)(2,1)S(1)}, u32[]{:S(2)}, u32[]{:S(2)}) %all-to-all-start.2) | async-done | bytes 57376 | tf_op jit(solution)/shard_map/all_to_all | solution.py:136
  219.8 27.5 %all_to_all.47 = bf16[16,3,7168]{2,1,0:T(4,128)(2,1)} all-to-all(bf16[16,3,7168]{2,1,0:T(4,128)(2,1)S(1)} %reshape.337), channel_id=1, replica_groups=mesh['ctx'=16,'exp'=16] {'exp'}, dimensions={0} | all-to-all | bytes 1376256 | tf_op jit(solution)/shard_map/all_to_all | solution.py:161
  247.3 2.3 all_to_all.37
  249.7 122.6 %all-gather.5.cloned.1.call-done = bf16[1,768,7168]{2,1,0:T(8,128)(2,1)} async-done(((bf16[1,48,7168]{2,1,0:T(8,128)(2,1)}), bf16[1,768,7168]{2,1,0:T(8,128)(2,1)}) %all-gather.5.cloned.1.call-update) | async-done | bytes 11010064 | tf_op jit(solution)/shard_map/all_gather | solution.py:169
  372.3 6.3 %fusion.2 = f32[768,128]{1,0:T(8,128)S(1)} fusion(bf16[1,768,7168]{2,1,0:T(8,128)(2,1)} %all-gather.5.cloned.1.call-done, bf16[1,7168,128]{2,1,0:T(8,128)(2,1)} %param.25), kind=kOutput, calls=%fused_computation.3 | convolution fusion | flops 1409286144 | bytes 13238272 | tf_op jit(solution)/shard_map/end,edf->enf/dot_general | solution.py:170
  378.7 17.3 %fusion.4 = bf16[768,1,7168]{2,0,1:T(8,128)(2,1)} fusion(bf16[1,128,7168]{2,1,0:T(8,128)(2,1)S(1)} %copy-done, bf16[1,7168,128]{2,1,0:T(8,128)(2,1)} %param.26, bf16[1,768,7168]{2,1,0:T(8,128)(2,1)} %all-gather.5.cloned.1.call-done, f32[768,128]{1,0:T(8,128)S(1)} %fusion.2), kind=kOutput, calls=%fused_computation.5 | convolution fusion | flops 2824667136 | bytes 26083328 | tf_op jit(solution)/shard_map/enf,efd->ned/dot_general | solution.py:174
  396.0 155.5 %reduce-scatter.2.cloned.1.call-done = bf16[48,1,7168]{2,0,1:T(8,128)(2,1)} async-done(((bf16[768,1,7168]{2,0,1:T(8,128)(2,1)}), bf16[48,1,7168]{2,0,1:T(8,128)(2,1)}) %reduce-scatter.2.cloned.1.call-update) | async-done | bytes 688144 | tf_op jit(solution)/shard_map/reduce_scatter | solution.py:173
  551.5 2.2 reshape.342
  553.7 4.5 all-to-all-start.4
  558.9 23.5 %all-to-all-done.4 = bf16[16,3,1,7168]{3,1,2,0:T(4,128)(2,1)S(1)} async-done(((bf16[16,3,1,7168]{3,1,2,0:T(4,128)(2,1)}), bf16[16,3,1,7168]{3,1,2,0:T(4,128)(2,1)S(1)}, u32[]{:S(2)}, u32[]{:S(2)}) %all-to-all-start.4) | async-done | bytes 688160 | tf_op jit(solution)/shard_map/all_to_all | solution.py:182
  (82 shorter events, 11.2 us)
Async XLA Ops:
  6.5 372.1 %copy-start = (bf16[1,128,7168]{2,1,0:T(8,128)(2,1)S(1)}, bf16[1,128,7168]{2,1,0:T(8,128)(2,1)}, u32[]{:S(2)}) copy-start(bf16[1,128,7168]{2,1,0:T(8,128)(2,1)} %param.27) | copy-start | bytes 5505028
  6.5 83.3 %all-gather.3.cloned.1.call-start = ((), (), s32[]{:S(2)}) async-start(), calls=%async_computation.6 | async-start | bytes 4177920 | tf_op jit(solution)/shard_map/all_gather | solution.py:118
  96.8 2.7 copy-start.1
  100.8 5.7 copy-start.2
  107.9 38.5 %copy-start.14 = (bf16[1024,448]{0,1:T(8,128)(2,1)S(1)}, bf16[1024,448]{0,1:T(8,128)(2,1)}, u32[]{:S(2)}) copy-start(bf16[1024,448]{0,1:T(8,128)(2,1)} %param.20) | copy-start | bytes 2752516
  147.9 26.7 %copy-start.12 = (s32[4,8]{1,0:T(4,128)S(1)}, s32[4,8]{1,0:T(4,128)}, u32[]{:S(2)}) copy-start(s32[4,8]{1,0:T(4,128)} %param.24) | copy-start | bytes 388
  147.9 70.1 %copy-start.3 = (bf16[4,7168]{1,0:T(4,128)(2,1)S(1)}, bf16[4,7168]{1,0:T(4,128)(2,1)}, u32[]{:S(2)}) copy-start(bf16[4,7168]{1,0:T(4,128)(2,1)} %param.21) | copy-start | bytes 172036
  147.9 70.3 %copy-start.9 = (f32[7168]{0:T(1024)S(1)}, f32[7168]{0:T(1024)}, u32[]{:S(2)}) copy-start(f32[7168]{0:T(1024)} %param.22) | copy-start | bytes 86020
  149.8 51.9 %all-to-all-start.1 = ((bf16[16,16,1,4,448]{4,3,1,2,0:T(4,128)(2,1)}), bf16[16,16,1,4,448]{4,3,1,2,0:T(4,128)(2,1)S(1)}, u32[]{:S(2)}, u32[]{:S(2)}) async-start(bf16[16,16,1,4,448]{4,3,1,2,0:T(4,128)(2,1)} %copy.43), calls=%async_computation.1 | async-start | bytes 2097152 | tf_op jit(solution)/shard_map/all_to_all | solution.py:37
  174.7 43.5 %copy-start.7 = (s32[4,16]{1,0:T(4,128)}, s32[4,16]{1,0:T(4,128)S(1)}, u32[]{:S(2)}) copy-start(s32[4,16]{1,0:T(4,128)S(1)} %convert_reduce_fusion) | copy-start | bytes 772
  202.8 15.0 %all-to-all-start.2 = ((bf16[16,1,4,448]{3,2,1,0:T(4,128)(2,1)}), bf16[16,1,4,448]{3,2,1,0:T(4,128)(2,1)S(1)}, u32[]{:S(2)}, u32[]{:S(2)}) async-start(bf16[16,1,4,448]{3,2,1,0:T(4,128)(2,1)} %bitcast.12), calls=%async_computation.2 | async-start | bytes 131072 | tf_op jit(solution)/shard_map/all_to_all | solution.py:136
  208.1 164.3 %all-gather.5.cloned.1.call-start = ((), (), s32[]{:S(2)}) async-start(), calls=%async_computation.7 | async-start | bytes 11698176 | tf_op jit(solution)/shard_map/all_gather | solution.py:169
  208.2 9.6 %copy-start.10 = (s32[4,16]{1,0:T(4,128)}, s32[4,16]{1,0:T(4,128)S(1)}, u32[]{:S(2)}) copy-start(s32[4,16]{1,0:T(4,128)S(1)} %sub.74) | copy-start | bytes 772
  218.3 0.6 copy-start.5
  249.7 301.8 %reduce-scatter.2.cloned.1.call-start = ((), (), s32[]{:S(2)}) async-start(), calls=%async_computation.8 | async-start | bytes 11698176 | tf_op jit(solution)/shard_map/reduce_scatter | solution.py:173
  396.0 162.2 %copy-start.8 = (s32[4,16]{1,0:T(4,128)S(1)}, s32[4,16]{1,0:T(4,128)}, u32[]{:S(2)}) copy-start(s32[4,16]{1,0:T(4,128)} %copy-done.7) | copy-start | bytes 772
  396.0 162.3 %copy-start.6 = (bf16[4,7168]{1,0:T(4,128)(2,1)S(1)}, bf16[4,7168]{1,0:T(4,128)(2,1)}, u32[]{:S(2)}) copy-start(bf16[4,7168]{1,0:T(4,128)(2,1)} %copy-done.5) | copy-start | bytes 172036
  396.0 162.3 %copy-start.15 = (bf16[7168,16]{0,1:T(8,128)(2,1)S(1)}, bf16[7168,16]{0,1:T(8,128)(2,1)}, u32[]{:S(2)}) copy-start(bf16[7168,16]{0,1:T(8,128)(2,1)} %param.23) | copy-start | bytes 688132
  396.0 162.5 %copy-start.13 = (s32[4,8]{1,0:T(4,128)S(1)}, s32[4,8]{1,0:T(4,128)}, u32[]{:S(2)}) copy-start(s32[4,8]{1,0:T(4,128)} %param.24) | copy-start | bytes 388
  396.0 162.8 %copy-start.11 = (s32[4,16]{1,0:T(4,128)S(1)}, s32[4,16]{1,0:T(4,128)}, u32[]{:S(2)}) copy-start(s32[4,16]{1,0:T(4,128)} %copy-done.10) | copy-start | bytes 772
  396.0 186.6 %copy-start.4 = (bf16[4,7168]{1,0:T(4,128)(2,1)S(1)}, bf16[4,7168]{1,0:T(4,128)(2,1)}, u32[]{:S(2)}) copy-start(bf16[4,7168]{1,0:T(4,128)(2,1)} %param.21) | copy-start | bytes 172036
  553.7 28.7 %all-to-all-start.4 = ((bf16[16,3,1,7168]{3,1,2,0:T(4,128)(2,1)}), bf16[16,3,1,7168]{3,1,2,0:T(4,128)(2,1)S(1)}, u32[]{:S(2)}, u32[]{:S(2)}) async-start(bf16[16,3,1,7168]{3,1,2,0:T(4,128)(2,1)} %bitcast.106), calls=%async_computation.5 | async-start | bytes 1835008 | tf_op jit(solution)/shard_map/all_to_all | solution.py:182
Sparse Core Ops, SparseCore 0:
  10.0 79.7 all-gather.2
  249.8 122.4 all-gather.4
  396.1 155.3 reduce-scatter.1
where the time goes:
time: 591 us; the launch traced here: 590 us
  waiting for transfers between devices  415 us (70%)
  blocking collectives  64.9 us (11%)
  matrix products  40.4 us (7%)
  starting transfers between devices  34.7 us (6%)
  local copies, waits for them, and re-layouts  14.9 us (3%)
  between operations  13.5 us (2%)
  other arithmetic  6.29 us (1%)
    reduce_scatter x1, waiting for transfers between devices, body(): lax.psum_scatter(jnp.einsum('enf,efd->ned', activations, w_down, preferre...  155 us
    all_gather x1, waiting for transfers between devices, body(): portion = lax.all_gather(arrived, 'ctx', axis=1, tiled=True)  123 us
    all_gather x1, waiting for transfers between devices, body(): portion = lax.all_gather(keys_here, 'ctx', axis=1, tiled=True)  77.7 us
    all_to_all x1, blocking collectives, copy_for_each(): return lax.all_to_all(copies, axis, split_axis=0, concat_axis=0, tiled=True)  37.4 us
    all_to_all x1, blocking collectives, body(): lax.all_to_all(send_rows.reshape(expert_count, CAP, model_width), 'exp',...  27.5 us
    all_to_all x1, waiting for transfers between devices, sum_at_owner(): lax.all_to_all(in_blocks(value, dim, length), axis, 0, 0, tiled=True)  27 us
    all_to_all x1, starting transfers between devices, sum_at_owner(): lax.all_to_all(in_blocks(value, dim, length), axis, 0, 0, tiled=True)  24.8 us
    all_to_all x1, waiting for transfers between devices, body(): lax.all_to_all(going_back, 'exp', split_axis=0, concat_axis=2, tiled=True)  23.5 us
  transfers between devices with their start and end apart: 6, of which 6 were waited for; matrix products, arithmetic and copies ran while one was open for 1% of the time, Pallas kernels for 0%

commit v1 on v0

--- a/solution.py
+++ b/solution.py
@@ -3,6 +3,7 @@
 import jax.numpy as jnp
 from jax import lax
 from jax.sharding import PartitionSpec as P
+from jax.lax import all_to_all, axis_size
 
 QKD = 192
 CAP = 3
@@ -166,7 +167,9 @@
         tiled=True,
     )
     local_experts = arrived.shape[0]
-    portion = lax.all_gather(arrived, "ctx", axis=1, tiled=True)
+    w1 = jnp.stack([arrived for _ in range(axis_size("ctx"))])
+    ready = all_to_all(w1, "ctx", 0, 0)
+    portion = jnp.concatenate(ready, axis=1)
     gate = jnp.einsum("end,edf->enf", portion, w_gate, preferred_element_type=jnp.float32)
     upward = jnp.einsum("end,edf->enf", portion, w_up, preferred_element_type=jnp.float32)
     activations = (jax.nn.silu(gate) * upward).astype(jnp.bfloat16)

time: 591 us -> 724 us (1.23)
  blocking collectives: 64.9 us -> 313 us
  waiting for transfers between devices: 415 us -> 295 us
  local copies, waits for them, and re-layouts: 14.9 us -> 23.8 us
    all_to_all x0 -> x1, blocking collectives: none -> 248 us  [body(): ready = all_to_all(w1, 'ctx', 0, 0)]
    all_gather x1 -> x0, waiting for transfers between devices: 123 us -> none  [body(): portion = lax.all_gather(arrived, 'ctx', axis=1, tiled=True)]
  transfers between devices with their start and end apart: 6 -> 5, of which waited for: 6 -> 5; matrix products, arithmetic and copies ran while one was open for 1% -> 1% of each run, Pallas kernels for 0% -> 0%
where the time goes in v1:
time: 724 us
  blocking collectives  313 us (43%)
  waiting for transfers between devices  295 us (41%)
  matrix products  37.2 us (5%)
  starting transfers between devices  34.7 us (5%)
  local copies, waits for them, and re-layouts  23.8 us (3%)
  between operations  13.8 us (2%)
    all_to_all x1, blocking collectives, body(): ready = all_to_all(w1, 'ctx', 0, 0)  248 us
    reduce_scatter x1, waiting for transfers between devices, body(): lax.psum_scatter(jnp.einsum('enf,efd->ned', activations, w_down, preferre...  157 us
    all_gather x1, waiting for transfers between devices, body(): portion = lax.all_gather(keys_here, 'ctx', axis=1, tiled=True)  77.7 us
    all_to_all x1, blocking collectives, copy_for_each(): return lax.all_to_all(copies, axis, split_axis=0, concat_axis=0, tiled=True)  37.4 us
    all_to_all x1, blocking collectives, body(): lax.all_to_all(send_rows.reshape(expert_count, CAP, model_width), 'exp',...  27.5 us
    all_to_all x1, waiting for transfers between devices, sum_at_owner(): lax.all_to_all(in_blocks(value, dim, length), axis, 0, 0, tiled=True)  27 us
    all_to_all x1, starting transfers between devices, sum_at_owner(): lax.all_to_all(in_blocks(value, dim, length), axis, 0, 0, tiled=True)  24.8 us
    all_to_all x1, waiting for transfers between devices, body(): lax.all_to_all(going_back, 'exp', split_axis=0, concat_axis=2, tiled=True)  23.5 us
  transfers between devices with their start and end apart: 5, of which 5 were waited for; matrix products, arithmetic and copies ran while one was open for 1% of the time, Pallas kernels for 0%

profile of v1, /device:TPU:1, one launch (start us, length us, event | category | flops | bytes accessed | tf_op | source)
XLA Modules:
  0.0 723.8 jit_solution(2725896101966155431)
XLA Ops:
  7.7 1.6 pad_maximum_fusion
  12.2 77.7 %all-gather.2.cloned.1.call-done = bf16[576,3072]{0,1:T(8,128)(2,1)} async-done(((bf16[576,192]{0,1:T(8,128)(2,1)}), bf16[576,3072]{0,1:T(8,128)(2,1)}) %all-gather.2.cloned.1.call-update) | async-done | bytes 3538960 | tf_op jit(solution)/shard_map/all_gather | solution.py:119
  89.8 3.9 fusion.9
  93.7 3.1 fusion.82
  96.8 2.6 copy-done.2
  100.8 5.6 fusion.35
  108.0 37.4 %all_to_all.48 = bf16[16,64,1024]{2,1,0:T(8,128)(2,1)S(1)} all-to-all(bf16[16,64,1024]{2,1,0:T(8,128)(2,1)S(1)} %broadcast_in_dim.120), channel_id=1, replica_groups=mesh['ctx'=16,'exp'=16] {'ctx'}, dimensions={0} | all-to-all | bytes 4194304 | tf_op jit(solution)/shard_map/all_to_all | solution.py:16
  146.5 1.4 fusion.22
  148.0 1.8 copy.43
  149.8 24.8 %all-to-all-start.1 = ((bf16[16,16,1,4,448]{4,3,1,2,0:T(4,128)(2,1)}), bf16[16,16,1,4,448]{4,3,1,2,0:T(4,128)(2,1)S(1)}, u32[]{:S(2)}, u32[]{:S(2)}) async-start(bf16[16,16,1,4,448]{4,3,1,2,0:T(4,128)(2,1)} %copy.43), calls=%async_computation.1 | async-start | bytes 2097152 | tf_op jit(solution)/shard_map/all_to_all | solution.py:38
  174.7 27.0 %all-to-all-done.1 = bf16[16,16,1,4,448]{4,3,1,2,0:T(4,128)(2,1)S(1)} async-done(((bf16[16,16,1,4,448]{4,3,1,2,0:T(4,128)(2,1)}), bf16[16,16,1,4,448]{4,3,1,2,0:T(4,128)(2,1)S(1)}, u32[]{:S(2)}, u32[]{:S(2)}) %all-to-all-start.1) | async-done | bytes 917536 | tf_op jit(solution)/shard_map/all_to_all | solution.py:38
  202.8 5.3 all-to-all-start.2
  208.6 9.2 %all-to-all-done.2 = bf16[16,1,4,448]{3,2,1,0:T(4,128)(2,1)S(1)} async-done(((bf16[16,1,4,448]{3,2,1,0:T(4,128)(2,1)}), bf16[16,1,4,448]{3,2,1,0:T(4,128)(2,1)S(1)}, u32[]{:S(2)}, u32[]{:S(2)}) %all-to-all-start.2) | async-done | bytes 57376 | tf_op jit(solution)/shard_map/all_to_all | solution.py:137
  219.8 27.5 %all_to_all.49 = bf16[16,3,7168]{2,1,0:T(4,128)(2,1)} all-to-all(bf16[16,3,7168]{2,1,0:T(4,128)(2,1)S(1)} %reshape.345), channel_id=1, replica_groups=mesh['ctx'=16,'exp'=16] {'exp'}, dimensions={0} | all-to-all | bytes 1376256 | tf_op jit(solution)/shard_map/all_to_all | solution.py:162
  247.3 1.6 stack.4
  249.0 5.5 stack.5
  254.5 248.3 %all_to_all.50 = bf16[16,1,48,7168]{3,2,1,0:T(8,128)(2,1)S(1)} all-to-all(bf16[16,1,48,7168]{3,2,1,0:T(8,128)(2,1)} %stack.5), channel_id=1, replica_groups=mesh['ctx'=16,'exp'=16] {'ctx'}, dimensions={0} | all-to-all | bytes 22020096 | tf_op jit(solution)/shard_map/all_to_all | solution.py:171
  502.8 4.0 copy-done.1
  506.9 3.0 fusion.17
  509.9 17.3 %fusion = bf16[768,1,7168]{2,0,1:T(8,128)(2,1)} fusion(bf16[1,128,7168]{2,1,0:T(8,128)(2,1)S(1)} %copy-done, bf16[768,7168]{1,0:T(8,128)(2,1)} %bitcast.99, bf16[1,7168,128]{2,1,0:T(8,128)(2,1)} %param.26, f32[768,128]{1,0:T(8,128)S(1)} %fusion.17), kind=kOutput, calls=%fused_computation.1 | convolution fusion | flops 2824667136 | bytes 26083328 | tf_op jit(solution)/shard_map/enf,efd->ned/dot_general | solution.py:177
  527.3 157.5 %reduce-scatter.2.cloned.1.call-done = bf16[48,1,7168]{2,0,1:T(8,128)(2,1)} async-done(((bf16[768,1,7168]{2,0,1:T(8,128)(2,1)}), bf16[48,1,7168]{2,0,1:T(8,128)(2,1)}) %reduce-scatter.2.cloned.1.call-update) | async-done | bytes 688144 | tf_op jit(solution)/shard_map/reduce_scatter | solution.py:176
  684.8 2.2 reshape.350
  687.0 4.5 all-to-all-start.5
  692.2 23.5 %all-to-all-done.5 = bf16[16,3,1,7168]{3,1,2,0:T(4,128)(2,1)S(1)} async-done(((bf16[16,3,1,7168]{3,1,2,0:T(4,128)(2,1)}), bf16[16,3,1,7168]{3,1,2,0:T(4,128)(2,1)S(1)}, u32[]{:S(2)}, u32[]{:S(2)}) %all-to-all-start.5) | async-done | bytes 688160 | tf_op jit(solution)/shard_map/all_to_all | solution.py:185
  (85 shorter events, 13.5 us)
Async XLA Ops:
  6.5 503.3 %copy-start = (bf16[1,128,7168]{2,1,0:T(8,128)(2,1)S(1)}, bf16[1,128,7168]{2,1,0:T(8,128)(2,1)}, u32[]{:S(2)}) copy-start(bf16[1,128,7168]{2,1,0:T(8,128)(2,1)} %param.27) | copy-start | bytes 5505028
  6.5 83.3 %all-gather.2.cloned.1.call-start = ((), (), s32[]{:S(2)}) async-start(), calls=%async_computation.7 | async-start | bytes 4177920 | tf_op jit(solution)/shard_map/all_gather | solution.py:119
  96.8 2.7 copy-start.2
  100.8 5.7 copy-start.3
  107.9 38.5 %copy-start.16 = (bf16[1024,448]{0,1:T(8,128)(2,1)S(1)}, bf16[1024,448]{0,1:T(8,128)(2,1)}, u32[]{:S(2)}) copy-start(bf16[1024,448]{0,1:T(8,128)(2,1)} %param.20) | copy-start | bytes 2752516
  147.9 26.7 %copy-start.13 = (s32[4,8]{1,0:T(4,128)S(1)}, s32[4,8]{1,0:T(4,128)}, u32[]{:S(2)}) copy-start(s32[4,8]{1,0:T(4,128)} %param.24) | copy-start | bytes 388
  147.9 70.1 %copy-start.4 = (bf16[4,7168]{1,0:T(4,128)(2,1)S(1)}, bf16[4,7168]{1,0:T(4,128)(2,1)}, u32[]{:S(2)}) copy-start(bf16[4,7168]{1,0:T(4,128)(2,1)} %param.21) | copy-start | bytes 172036
  147.9 70.3 %copy-start.10 = (f32[7168]{0:T(1024)S(1)}, f32[7168]{0:T(1024)}, u32[]{:S(2)}) copy-start(f32[7168]{0:T(1024)} %param.22) | copy-start | bytes 86020
  149.8 51.9 %all-to-all-start.1 = ((bf16[16,16,1,4,448]{4,3,1,2,0:T(4,128)(2,1)}), bf16[16,16,1,4,448]{4,3,1,2,0:T(4,128)(2,1)S(1)}, u32[]{:S(2)}, u32[]{:S(2)}) async-start(bf16[16,16,1,4,448]{4,3,1,2,0:T(4,128)(2,1)} %copy.43), calls=%async_computation.1 | async-start | bytes 2097152 | tf_op jit(solution)/shard_map/all_to_all | solution.py:38
  174.7 43.5 %copy-start.8 = (s32[4,16]{1,0:T(4,128)}, s32[4,16]{1,0:T(4,128)S(1)}, u32[]{:S(2)}) copy-start(s32[4,16]{1,0:T(4,128)S(1)} %convert_reduce_fusion) | copy-start | bytes 772
  202.8 15.0 %all-to-all-start.2 = ((bf16[16,1,4,448]{3,2,1,0:T(4,128)(2,1)}), bf16[16,1,4,448]{3,2,1,0:T(4,128)(2,1)S(1)}, u32[]{:S(2)}, u32[]{:S(2)}) async-start(bf16[16,1,4,448]{3,2,1,0:T(4,128)(2,1)} %bitcast.12), calls=%async_computation.2 | async-start | bytes 131072 | tf_op jit(solution)/shard_map/all_to_all | solution.py:137
  208.1 476.7 %reduce-scatter.2.cloned.1.call-start = ((), (), s32[]{:S(2)}) async-start(), calls=%async_computation.8 | async-start | bytes 11698176 | tf_op jit(solution)/shard_map/reduce_scatter | solution.py:176
  208.2 9.6 %copy-start.11 = (s32[4,16]{1,0:T(4,128)}, s32[4,16]{1,0:T(4,128)S(1)}, u32[]{:S(2)}) copy-start(s32[4,16]{1,0:T(4,128)S(1)} %sub.74) | copy-start | bytes 772
  218.3 0.6 copy-start.6
  254.5 252.4 %copy-start.15 = (bf16[1,7168,128]{2,1,0:T(8,128)(2,1)S(1)}, bf16[1,7168,128]{2,1,0:T(8,128)(2,1)}, u32[]{:S(2)}) copy-start(bf16[1,7168,128]{2,1,0:T(8,128)(2,1)} %param.25) | copy-start | bytes 5505028
  502.8 4.0 copy-start.1
  527.2 164.3 %copy-start.9 = (s32[4,16]{1,0:T(4,128)S(1)}, s32[4,16]{1,0:T(4,128)}, u32[]{:S(2)}) copy-start(s32[4,16]{1,0:T(4,128)} %copy-done.8) | copy-start | bytes 772
  527.2 164.3 %copy-start.7 = (bf16[4,7168]{1,0:T(4,128)(2,1)S(1)}, bf16[4,7168]{1,0:T(4,128)(2,1)}, u32[]{:S(2)}) copy-start(bf16[4,7168]{1,0:T(4,128)(2,1)} %copy-done.6) | copy-start | bytes 172036
  527.2 164.3 %copy-start.17 = (bf16[7168,16]{0,1:T(8,128)(2,1)S(1)}, bf16[7168,16]{0,1:T(8,128)(2,1)}, u32[]{:S(2)}) copy-start(bf16[7168,16]{0,1:T(8,128)(2,1)} %param.23) | copy-start | bytes 688132
  527.2 164.5 %copy-start.14 = (s32[4,8]{1,0:T(4,128)S(1)}, s32[4,8]{1,0:T(4,128)}, u32[]{:S(2)}) copy-start(s32[4,8]{1,0:T(4,128)} %param.24) | copy-start | bytes 388
  527.2 164.8 %copy-start.12 = (s32[4,16]{1,0:T(4,128)S(1)}, s32[4,16]{1,0:T(4,128)}, u32[]{:S(2)}) copy-start(s32[4,16]{1,0:T(4,128)} %copy-done.11) | copy-start | bytes 772
  527.3 188.7 %copy-start.5 = (bf16[4,7168]{1,0:T(4,128)(2,1)S(1)}, bf16[4,7168]{1,0:T(4,128)(2,1)}, u32[]{:S(2)}) copy-start(bf16[4,7168]{1,0:T(4,128)(2,1)} %param.21) | copy-start | bytes 172036
  687.0 28.7 %all-to-all-start.5 = ((bf16[16,3,1,7168]{3,1,2,0:T(4,128)(2,1)}), bf16[16,3,1,7168]{3,1,2,0:T(4,128)(2,1)S(1)}, u32[]{:S(2)}, u32[]{:S(2)}) async-start(bf16[16,3,1,7168]{3,1,2,0:T(4,128)(2,1)} %bitcast.100), calls=%async_computation.6 | async-start | bytes 1835008 | tf_op jit(solution)/shard_map/all_to_all | solution.py:185
Sparse Core Ops, SparseCore 0:
  10.0 79.7 all-gather.1
  527.4 157.3 reduce-scatter.1
